TPU v7x, 32 devices: a whole 2x2x4 slice. The times are simulated.
32 devices in a mesh: tp: 8 (over z, core), seq: 4 (over y, x).
Axes of the slice: x: 2, y: 2, z: 4, core: 2. Of those that a mesh axis runs over, the one named last changes fastest.
Arguments:
- residual: bfloat16 [1024, 4096], P('seq'), may hold values from -6 to 6
- mix_gain: float32 [4096], replicated, may hold values from 0.5 to 1.5
- in_proj: bfloat16 [4096, 4096], P(None, 'tp'), may hold values from -0.09375 to 0.09375
- branch_proj: bfloat16 [4096, 4096], P(None, 'tp'), may hold values from -0.09375 to 0.09375
- conv_weight: float32 [4, 4096], P(None, 'tp'), may hold values from -3 to 3
- conv_bias: float32 [4096], P('tp'), may hold values from -1.25 to 1.25
- input_gate: bfloat16 [16, 256, 256], P('tp'), may hold values from -0.375 to 0.375
- input_bias: float32 [4096], P('tp'), may hold values from -3 to 3
- decay_gate: bfloat16 [16, 256, 256], P('tp'), may hold values from -0.375 to 0.375
- decay_bias: float32 [4096], P('tp'), may hold values from -3 to 3
- decay_param: float32 [4096], P('tp'), may hold values from -13 to -2, as said below
- out_proj: bfloat16 [4096, 4096], P('tp'), may hold values from -0.25 to 0.25
- mlp_gain: float32 [4096], replicated, may hold values from 0.5 to 1.5
- gate_proj: bfloat16 [4096, 12288], P('seq', 'tp'), may hold values from -0.09375 to 0.09375
- up_proj: bfloat16 [4096, 12288], P('seq', 'tp'), may hold values from -0.09375 to 0.09375
- down_proj: bfloat16 [12288, 4096], P('tp'), may hold values from -0.078125 to 0.078125
Outputs:
- updated: bfloat16 [1024, 4096], P('seq')
Inputs may be any that keep to these rules, and one draw needn't show every extreme that they name: softplus(decay_param) lies between 0.02 / 1024 and 0.1 for every channel.
All inputs are finite; a program needn't handle non-finite values.
Results may differ from a plain program's by a relative error of at most 0.02.
Values may be sent and summed in bfloat16 or wider, within the bound.
A program may use at most 128 MiB of HBM per device.

v0:
```python
import jax
import jax.numpy as jnp
from jax import lax
from jax.sharding import PartitionSpec as P

epsilon = 1e-06


def from_behind(value, axis, steps):
    count = lax.axis_size(axis)
    leading, last = (max(0, -steps), min(count, count - steps))
    return lax.ppermute(value, axis, [(source, source + steps) for source in range(leading, last)])


def carried_in(shard, axis, combine, identity, reverse):
    count, mine = (lax.axis_size(axis), lax.axis_index(axis))
    everything = jax.tree.map(lambda part: lax.all_gather(part, axis), shard)
    start = jax.tree.map(
        lambda part, zero: jnp.broadcast_to(jnp.asarray(zero, part.dtype), part.shape),
        shard,
        identity,
    )

    def lap(k, before):
        at = count - 1 - k if reverse else k
        reached = at > mine if reverse else at < mine
        new = combine(before, jax.tree.map(lambda part: part[at], everything))
        return jax.tree.map(lambda a, b: jnp.where(reached, a, b), new, before)

    return lax.fori_loop(0, count, lap, start)


def summed_rows(product, extent, axis):
    everything = product(jnp.int32(0), lax.axis_size(axis) * extent)
    own = lax.psum_scatter(everything.astype(jnp.bfloat16), axis, scatter_dimension=0, tiled=True)
    return own.astype(jnp.float32)


def rms_norm(values, gain):
    wide = values.astype(jnp.float32)
    factor = lax.rsqrt(jnp.mean(wide * wide, axis=-1, keepdims=True) + epsilon)
    return (wide * factor * gain).astype(jnp.bfloat16)


def block_gates(values, weight, bias):
    heads, width = (weight.shape[0], weight.shape[1])
    grouped = values.reshape(values.shape[0], heads, width)
    mixed = jnp.einsum("thi,hij->thj", grouped, weight, preferred_element_type=jnp.float32)
    return jax.nn.sigmoid(mixed.reshape(values.shape[0], heads * width) + bias)


def smooth(inner, tail, conv_weight, conv_bias):
    taps = conv_weight.shape[0]
    length = inner.shape[0]
    padded = jnp.concatenate([tail, inner], axis=0).astype(jnp.float32)
    total = conv_bias + jnp.zeros((length, inner.shape[1]), jnp.float32)
    for offset in range(taps):
        total = total + conv_weight[offset] * padded[taps - 1 - offset : taps - 1 - offset + length]
    return lax.optimization_barrier(total.astype(jnp.bfloat16))


def combine_state(earlier, later):
    return (earlier[0] * later[0], later[0] * earlier[1] + later[1])


def channel_total(partial_value):
    return lax.psum(partial_value.astype(jnp.bfloat16), "tp").astype(jnp.float32)


def on_device(
    residual,
    mix_gain,
    in_proj,
    branch_proj,
    conv_weight,
    conv_bias,
    input_gate,
    input_bias,
    decay_gate,
    decay_bias,
    decay_param,
    out_proj,
    mlp_gain,
    gate_proj,
    up_proj,
    down_proj,
):
    length = residual.shape[0]
    taps = conv_weight.shape[0]
    normed = rms_norm(residual, mix_gain)
    branch = jax.nn.gelu(
        jnp.dot(normed, branch_proj, preferred_element_type=jnp.float32), approximate=True
    )
    inner = jnp.dot(normed, in_proj, preferred_element_type=jnp.float32).astype(jnp.bfloat16)
    tail = from_behind(inner[length - (taps - 1) :], "seq", 1)
    smoothed = smooth(inner, tail, conv_weight, conv_bias)
    input_rate = block_gates(smoothed, input_gate, input_bias)
    decay_rate = block_gates(smoothed, decay_gate, decay_bias)
    log_decay = -8.0 * decay_rate * jax.nn.softplus(decay_param)
    decay = jnp.exp(log_decay)
    position = lax.axis_index("seq")
    first = jnp.logical_and(position == 0, jnp.arange(length) == 0)[:, None]
    scale_in = jnp.where(first, 1.0, jnp.sqrt(-jnp.expm1(2.0 * log_decay)))
    pushed = smoothed.astype(jnp.float32) * input_rate * scale_in
    decays, partial_states = lax.associative_scan(combine_state, (decay, pushed), axis=0)
    end_decay = decays[-1]
    end_state = partial_states[-1]
    carried = carried_in(
        (end_decay, end_state),
        "seq",
        combine_state,
        (jnp.ones_like(end_decay), jnp.zeros_like(end_state)),
        False,
    )[1]
    states = partial_states + decays * carried[None]
    gated = (states * branch).astype(jnp.bfloat16)
    mixed = channel_total(jnp.dot(gated, out_proj, preferred_element_type=jnp.float32))
    middle = lax.optimization_barrier((residual.astype(jnp.float32) + mixed).astype(jnp.bfloat16))
    hidden_in = rms_norm(middle, mlp_gain)
    width = gate_proj.shape[1]
    columns = lax.all_to_all(hidden_in, "seq", split_axis=1, concat_axis=0, tiled=True)

    def term(start, count):
        block = lax.dynamic_slice_in_dim(columns, start, count, 0)
        return jnp.concatenate(
            [
                jnp.dot(block, gate_proj, preferred_element_type=jnp.float32),
                jnp.dot(block, up_proj, preferred_element_type=jnp.float32),
            ],
            axis=1,
        )

    joined = summed_rows(term, length, "seq")
    gate = joined[:, :width]
    up = joined[:, width:]
    hidden = (jax.nn.gelu(gate, approximate=True) * up).astype(jnp.bfloat16)
    output = channel_total(jnp.dot(hidden, down_proj, preferred_element_type=jnp.float32))
    return (middle.astype(jnp.float32) + output).astype(jnp.bfloat16)


def solution(mesh):
    in_specs = (
        P("seq", None),
        P(),
        P(None, "tp"),
        P(None, "tp"),
        P(None, "tp"),
        P("tp"),
        P("tp", None, None),
        P("tp"),
        P("tp", None, None),
        P("tp"),
        P("tp"),
        P("tp", None),
        P(),
        P("seq", "tp"),
        P("seq", "tp"),
        P("tp", None),
    )
    out_specs = P("seq", None)
    return jax.shard_map(
        on_device, mesh=mesh, in_specs=in_specs, out_specs=out_specs, check_vma=False
    )
```

profile of v0, /device:TPU:0, one launch (start us, length us, event | category | flops | bytes accessed | tf_op | source)
XLA Modules:
  0.0 392.3 jit_solution(13531175450782179382)
XLA Ops:
  6.5 2.2 fusion
  8.8 4.1 %convolution_convert_fusion.4 = bf16[256,512]{1,0:T(8,128)(2,1)S(1)} fusion(bf16[4096,512]{1,0:T(8,128)(2,1)} %param.20, bf16[256,4096]{1,0:T(8,128)(2,1)} %param.18, f32[4096]{0:T(1024)} %param.19, f32[256]{0:T(256)S(1)} %add_rsqrt_fusion.1), kind=kOutput, calls=%fused_computation.33 | convolution fusion | flops 1078067200 | bytes 6571008 | tf_op jit(solution)/shard_map/dot_general | solution.py:94
  13.0 4.9 %collective-permute-start = (bf16[3,512]{1,0:T(4,128)(2,1)S(1)}, bf16[3,512]{1,0:T(4,128)(2,1)S(1)}, u32[]{:S(2)}, u32[]{:S(2)}) collective-permute-start(bf16[3,512]{1,0:T(4,128)(2,1)S(1)} %slice.356), channel_id=1, source_target_pairs={{0,1},{1,2},{2,3},{4,5},{5,6},{6,7},{8,9},{9,10},{10,11},{12,13},{... | collective-permute-start | bytes 9224 | tf_op jit(solution)/shard_map/ppermute | solution.py:12
  18.0 1.2 collective-permute-done
  19.6 1.1 fusion.51
  20.6 2.1 copy.40
  22.7 2.0 fusion.53
  24.7 2.0 copy.39
  26.8 2.6 select_multiply_fusion
  29.4 0.8 copy-done.3
  30.1 2.5 slice.336
  32.7 2.5 slice.282
  35.1 2.5 slice.281
  37.6 0.7 slice.387
  38.3 2.5 slice.284
  40.8 2.5 slice.280
  43.3 2.5 slice.279
  45.8 1.3 multiply_add_fusion
  47.1 0.7 copy-done.4
  47.8 1.6 slice.334
  49.4 1.0 slice.288
  50.4 1.6 slice.287
  52.6 0.7 slice.290
  53.3 0.7 slice.286
  54.0 0.8 slice.285
  54.8 1.1 multiply_add_fusion.1
  62.4 0.8 fusion.66
  63.2 0.7 pad_maximum_fusion.8
  64.6 0.8 pad.123
  68.0 0.9 pad_maximum_fusion.5
  68.9 0.9 pad.109
  69.8 2.2 pad.125
  72.0 1.6 add.316
  74.2 1.7 fusion.63
  76.7 0.9 pad_maximum_fusion.3
  77.6 1.4 pad.110
  79.0 2.3 pad.111
  81.4 2.4 pad.127
  83.7 1.7 add.317
  85.4 1.8 add.308
  87.2 2.1 fusion.55
  89.3 0.7 pad_maximum_fusion.2
  90.1 2.6 pad.128
  92.7 1.7 pad_maximum_fusion.1
  94.3 2.6 pad.112
  97.0 2.6 pad.113
  99.6 0.7 add_bitcast_fusion
  100.3 9.8 %all-gather.1 = f32[4,1,512]{2,1,0:T(1,128)S(1)} all-gather(f32[1,1,512]{2,1,0:T(1,128)S(1)} %add_bitcast_fusion), channel_id=1, replica_groups=mesh['tp'=8,'seq'=4] {'seq'}, dimensions={0}, use_global_device_ids=true | all-gather | bytes 10240 | tf_op jit(solution)/shard_map/all_gather | solution.py:17
  110.1 1.7 pad.129
  111.8 0.7 add_bitcast_fusion.1
  112.5 7.2 %all-gather = f32[4,1,512]{2,1,0:T(1,128)S(1)} all-gather(f32[1,1,512]{2,1,0:T(1,128)S(1)} %add_bitcast_fusion.1), channel_id=1, replica_groups=mesh['tp'=8,'seq'=4] {'seq'}, dimensions={0}, use_global_device_ids=true | all-gather | bytes 10240 | tf_op jit(solution)/shard_map/all_gather | solution.py:17
  119.9 8.6 %convolution_convert_fusion.1 = bf16[256,4096]{1,0:T(8,128)(2,1)} fusion(bf16[512,4096]{1,0:T(8,128)(2,1)} %param.29, bf16[4096,512]{1,0:T(8,128)(2,1)} %param.21, bf16[256,4096]{1,0:T(8,128)(2,1)} %param.18, f32[4096]{0:T(1024)S(1)} %copy-done.18, f32[256]{0:T(256)S(1)} %copy-done.16, f32[256,512]{1,0:T(8,128)} %pad.128, f32[256,512]{1,0:T(8,128)} %pad.129, ...), kind=kOutput, calls=%fused_computation.11 | convolution fusion | flops 2154561536 | bytes 14699520 | tf_op jit(solution)/shard_map/dot_general | solution.py:117
  128.7 65.5 %all-reduce.35.cloned.1.call-done = bf16[256,4096]{1,0:T(8,128)(2,1)} async-done(((bf16[256,4096]{1,0:T(8,128)(2,1)}), bf16[256,4096]{1,0:T(8,128)(2,1)}) %all-reduce.35.cloned.1.call-update) | async-done | bytes 2097168 | tf_op jit(solution)/shard_map/psum | solution.py:67
  194.1 3.0 fusion.3
  197.7 0.7 fusion.6
  198.7 27.4 %all_to_all.19 = bf16[256,4,1024]{2,0,1:T(8,128)(2,1)S(1)} all-to-all(bf16[256,4,1024]{2,0,1:T(8,128)(2,1)S(1)} %bitcast.50), channel_id=1, replica_groups=mesh['tp'=8,'seq'=4] {'seq'}, dimensions={1} | all-to-all | bytes 4194304 | tf_op jit(solution)/shard_map/all_to_all | solution.py:121
  226.1 3.6 convolution_convert_fusion.2
  229.7 3.6 convolution_convert_fusion.3
  233.4 3.6 pad_maximum_fusion
  237.0 67.9 %reduce-scatter.2.cloned.1.call-done = bf16[256,3072]{1,0:T(8,128)(2,1)} async-done(((bf16[1024,3072]{1,0:T(8,128)(2,1)}), bf16[256,3072]{1,0:T(8,128)(2,1)}) %reduce-scatter.2.cloned.1.call-update) | async-done | bytes 1572880 | tf_op jit(solution)/shard_map/reduce_scatter | solution.py:35
  304.9 1.8 convert_element_type.66
  306.7 9.4 %convolution_convert_fusion = bf16[256,4096]{1,0:T(8,128)(2,1)} fusion(bf16[1536,4096]{1,0:T(8,128)(2,1)} %param.33, f32[256,3072]{1,0:T(8,128)S(1)} %convert_element_type.66), kind=kOutput, calls=%fused_computation.10 | convolution fusion | flops 3226206208 | bytes 17825792 | tf_op jit(solution)/shard_map/dot_general | solution.py:137
  316.1 65.3 %all-reduce.37.cloned.1.call-done = bf16[256,4096]{1,0:T(8,128)(2,1)} async-done(((bf16[256,4096]{1,0:T(8,128)(2,1)}), bf16[256,4096]{1,0:T(8,128)(2,1)}) %all-reduce.37.cloned.1.call-update) | async-done | bytes 2097168 | tf_op jit(solution)/shard_map/psum | solution.py:67
  381.4 4.3 %fusion.7 = bf16[256,4096]{1,0:T(8,128)(2,1)} fusion(bf16[256,4096]{1,0:T(8,128)(2,1)} %copy-done.2, bf16[256,4096]{1,0:T(8,128)(2,1)} %all-reduce.37.cloned.1.call-done), kind=kLoop, calls=%fused_computation.19 | loop fusion | flops 4194304 | bytes 6291456 | tf_op jit(solution)/shard_map/convert_element_type | solution.py:138
  (149 shorter events, 13.3 us)
Async XLA Ops:
  6.5 219.5 %copy-start = (bf16[1024,1536]{1,0:T(8,128)(2,1)S(1)}, bf16[1024,1536]{1,0:T(8,128)(2,1)}, u32[]{:S(2)}) copy-start(bf16[1024,1536]{1,0:T(8,128)(2,1)} %param.32) | copy-start | bytes 9437188
  6.5 187.6 %all-reduce.35.cloned.1.call-start = ((), (), s32[]{:S(2)}) async-start(), calls=%async_computation.2 | async-start | bytes 4194304 | tf_op jit(solution)/shard_map/psum | solution.py:67
  8.8 4.2 %copy-start.15 = (f32[256]{0:T(256)}, f32[256]{0:T(256)S(1)}, u32[]{:S(2)}) copy-start(f32[256]{0:T(256)S(1)} %add_rsqrt_fusion.1) | copy-start | bytes 3076
  8.8 9.1 %copy-start.13 = (f32[512]{0:T(512)S(1)}, f32[512]{0:T(512)}, u32[]{:S(2)}) copy-start(f32[512]{0:T(512)} %param.28) | copy-start | bytes 6148
  8.8 9.1 %copy-start.10 = (f32[4,512]{1,0:T(4,128)S(1)}, f32[4,512]{1,0:T(4,128)}, u32[]{:S(2)}) copy-start(f32[4,512]{1,0:T(4,128)} %param.22) | copy-start | bytes 24580
  8.8 10.5 %copy-start.14 = (f32[512]{0:T(512)S(1)}, f32[512]{0:T(512)}, u32[]{:S(2)}) copy-start(f32[512]{0:T(512)} %param.23) | copy-start | bytes 6148
  13.0 6.2 %collective-permute-start = (bf16[3,512]{1,0:T(4,128)(2,1)S(1)}, bf16[3,512]{1,0:T(4,128)(2,1)S(1)}, u32[]{:S(2)}, u32[]{:S(2)}) collective-permute-start(bf16[3,512]{1,0:T(4,128)(2,1)S(1)} %slice.356), channel_id=1, source_target_pairs={{0,1},{1,2},{2,3},{4,5},{5,6},{6,7},{8,9},{9,10},{10,11},{12,13},{... | collective-permute-start | bytes 9224 | tf_op jit(solution)/shard_map/ppermute | solution.py:12
  18.0 1.6 copy-start.6
  19.3 7.5 %copy-start.11 = (f32[512]{0:T(512)S(1)}, f32[512]{0:T(512)}, u32[]{:S(2)}) copy-start(f32[512]{0:T(512)} %param.25) | copy-start | bytes 6148
  19.3 7.5 %copy-start.12 = (f32[512]{0:T(512)S(1)}, f32[512]{0:T(512)}, u32[]{:S(2)}) copy-start(f32[512]{0:T(512)} %param.27) | copy-start | bytes 6148
  29.4 0.8 copy-start.3
  47.1 0.7 copy-start.4
  58.4 8.2 %copy-start.7 = (f32[31,512]{1,0:T(8,128)S(1)}, f32[31,512]{1,0:T(8,128)}, u32[]{:S(2)}) copy-start(f32[31,512]{1,0:T(8,128)} %slice.332) | copy-start | bytes 190468
  58.5 8.2 %copy-start.8 = (f32[31,512]{1,0:T(8,128)S(1)}, f32[31,512]{1,0:T(8,128)}, u32[]{:S(2)}) copy-start(f32[31,512]{1,0:T(8,128)} %slice.291) | copy-start | bytes 190468
  87.2 32.7 %copy-start.16 = (f32[256]{0:T(256)S(1)}, f32[256]{0:T(256)}, u32[]{:S(2)}) copy-start(f32[256]{0:T(256)} %copy-done.15) | copy-start | bytes 3076
  87.2 32.7 %copy-start.18 = (f32[4096]{0:T(1024)S(1)}, f32[4096]{0:T(1024)}, u32[]{:S(2)}) copy-start(f32[4096]{0:T(1024)} %param.19) | copy-start | bytes 49156
  89.3 20.8 %copy-start.5 = (f32[128,512]{1,0:T(8,128)S(1)}, f32[128,512]{1,0:T(8,128)}, u32[]{:S(2)}) copy-start(f32[128,512]{1,0:T(8,128)} %add.317) | copy-start | bytes 786436
  128.6 69.1 %copy-start.9 = (f32[4096]{0:T(1024)S(1)}, f32[4096]{0:T(1024)}, u32[]{:S(2)}) copy-start(f32[4096]{0:T(1024)} %param.30) | copy-start | bytes 49156
  128.6 176.3 %reduce-scatter.2.cloned.1.call-start = ((), (), s32[]{:S(2)}) async-start(), calls=%async_computation.3 | async-start | bytes 7864320 | tf_op jit(solution)/shard_map/reduce_scatter | solution.py:35
  197.1 1.3 copy-start.2
  226.1 3.6 copy-start.17
  237.0 144.5 %all-reduce.37.cloned.1.call-start = ((), (), s32[]{:S(2)}) async-start(), calls=%async_computation.4 | async-start | bytes 4194304 | tf_op jit(solution)/shard_map/psum | solution.py:67
  316.1 69.6 %copy-start.1 = (bf16[1024,1536]{1,0:T(8,128)(2,1)S(1)}, bf16[1024,1536]{1,0:T(8,128)(2,1)}, u32[]{:S(2)}) copy-start(bf16[1024,1536]{1,0:T(8,128)(2,1)} %param.32) | copy-start | bytes 9437188
Sparse Core Ops, SparseCore 0:
  128.7 65.3 all-reduce.34
  237.1 67.7 reduce-scatter.1
  316.3 65.1 all-reduce.36
where the time goes:
time: 394 us; the launch traced here: 392 us
  waiting for transfers between devices  200 us (51%)
  local copies, waits for them, and re-layouts  53.7 us (14%)
  blocking collectives  44.3 us (11%)
  other arithmetic  43 us (11%)
  matrix products  32.6 us (8%)
  between operations  13.7 us (3%)
  starting transfers between devices  4.96 us (1%)
    psum x2, waiting for transfers between devices, channel_total(): lax.psum(partial_value.astype(jnp.bfloat16), 'tp').astype(jnp.float32)  131 us
    reduce_scatter x1, waiting for transfers between devices, summed_rows(): lax.psum_scatter(everything.astype(jnp.bfloat16), axis, scatter_dimension...  67.9 us
    slice x52, local copies, waits for them, and re-layouts, on_device(): lax.associative_scan(combine_state, (decay, pushed), axis=0)  28 us
    all_to_all x1, blocking collectives, on_device(): lax.all_to_all(hidden_in, 'seq', split_axis=1, concat_axis=0, tiled=True)  27.4 us
    pad x28, local copies, waits for them, and re-layouts, on_device(): lax.associative_scan(combine_state, (decay, pushed), axis=0)  19.7 us
    all_gather x2, blocking collectives, carried_in(): everything = jax.tree.map(lambda part: lax.all_gather(part, axis), shard)  16.9 us
    dot_general x1, matrix products, on_device(): jnp.dot(hidden, down_proj, preferred_element_type=jnp.float32)  9.43 us
    dot_general x1, matrix products, on_device(): jnp.dot(gated, out_proj, preferred_element_type=jnp.float32)  8.64 us
  transfers between devices with their start and end apart: 4, of which 4 were waited for; matrix products, arithmetic and copies ran while one was open for 0% of the time, Pallas kernels for 0%

commit v1 on v0

--- a/solution.py
+++ b/solution.py
@@ -64,7 +64,9 @@
 
 
 def channel_total(partial_value):
-    return lax.psum(partial_value.astype(jnp.bfloat16), "tp").astype(jnp.float32)
+    return jnp.sum(lax.all_gather(partial_value.astype(jnp.bfloat16), "tp"), axis=0).astype(
+        jnp.float32
+    )
 
 
 def on_device(

time: 394 us -> 601 us (1.53)
  waiting for transfers between devices: 200 us -> 371 us
  other arithmetic: 43 us -> 65.3 us
  local copies, waits for them, and re-layouts: 53.7 us -> 62.4 us
    all_gather x0 -> x2, waiting for transfers between devices: none -> 302 us  [channel_total(): lax.all_gather(partial_value.astype(jnp.bfloat16), 'tp')]
    psum x2 -> x0, waiting for transfers between devices: 131 us -> none  [channel_total(): lax.psum(partial_value.astype(jnp.bfloat16), 'tp').astype(jnp.float32)]
    reduce_sum x0 -> x2, other arithmetic: none -> 21.1 us  [channel_total(): jnp.sum(lax.all_gather(partial_value.astype(jnp.bfloat16), 'tp'), axis=0)]
where the time goes in v1:
time: 601 us; the launch traced here: 599 us
  waiting for transfers between devices  371 us (62%)
  other arithmetic  65.3 us (11%)
  local copies, waits for them, and re-layouts  62.4 us (10%)
  blocking collectives  47.5 us (8%)
  matrix products  34.3 us (6%)
  between operations  13.7 us (2%)
    all_gather x2, waiting for transfers between devices, channel_total(): lax.all_gather(partial_value.astype(jnp.bfloat16), 'tp')  302 us
    reduce_scatter x1, waiting for transfers between devices, summed_rows(): lax.psum_scatter(everything.astype(jnp.bfloat16), axis, scatter_dimension...  66.9 us
    all_to_all x1, blocking collectives, on_device(): lax.all_to_all(hidden_in, 'seq', split_axis=1, concat_axis=0, tiled=True)  30.5 us
    slice x52, local copies, waits for them, and re-layouts, on_device(): lax.associative_scan(combine_state, (decay, pushed), axis=0)  28.1 us
    reduce_sum x2, other arithmetic, channel_total(): jnp.sum(lax.all_gather(partial_value.astype(jnp.bfloat16), 'tp'), axis=0)  21.1 us
    pad x28, local copies, waits for them, and re-layouts, on_device(): lax.associative_scan(combine_state, (decay, pushed), axis=0)  19.8 us
    all_gather x2, blocking collectives, carried_in(): everything = jax.tree.map(lambda part: lax.all_gather(part, axis), shard)  16.9 us
  transfers between devices with their start and end apart: 4, of which 4 were waited for; matrix products, arithmetic and copies ran while one was open for 0% of the time, Pallas kernels for 0%

profile of v1, /device:TPU:0, one launch (start us, length us, event | category | flops | bytes accessed | tf_op | source)
XLA Modules:
  0.0 599.1 jit_solution(10118021007132768531)
XLA Ops:
  6.5 2.2 fusion
  8.8 4.1 convolution_convert_fusion.4
  13.0 4.9 collective-permute-start
  18.0 1.2 collective-permute-done
  19.6 1.1 fusion.51
  20.6 2.1 copy.49
  22.7 2.0 fusion.53
  24.7 2.0 copy.48
  26.8 2.6 select_multiply_fusion
  29.4 0.8 copy-done.3
  30.2 2.5 slice.336
  32.7 2.5 slice.282
  35.2 2.5 slice.281
  38.4 2.5 slice.284
  40.9 2.5 slice.280
  43.4 2.5 slice.279
  45.9 1.3 multiply_add_fusion
  47.9 1.6 slice.334
  49.5 1.0 slice.288
  50.5 1.6 slice.287
  54.1 0.8 slice.285
  54.9 1.1 multiply_add_fusion.1
  62.5 0.8 fusion.66
  64.7 0.8 pad.123
  68.1 0.9 pad_maximum_fusion.5
  69.0 0.9 pad.109
  69.9 2.2 pad.125
  72.0 1.6 add.312
  74.3 1.7 fusion.63
  76.7 0.9 pad_maximum_fusion.3
  77.7 1.5 pad.110
  79.1 2.3 pad.111
  81.4 2.4 pad.127
  83.8 1.7 add.313
  85.5 1.8 add.304
  87.3 2.1 fusion.55
  89.4 0.7 pad_maximum_fusion.2
  90.1 2.6 pad.128
  92.8 1.7 pad_maximum_fusion.1
  94.4 2.6 pad.112
  97.1 2.6 pad.113
  99.7 0.7 add_bitcast_fusion
  100.4 9.8 %all-gather.3 = f32[4,1,512]{2,1,0:T(1,128)S(1)} all-gather(f32[1,1,512]{2,1,0:T(1,128)S(1)} %add_bitcast_fusion), channel_id=1, replica_groups=mesh['tp'=8,'seq'=4] {'seq'}, dimensions={0}, use_global_device_ids=true | all-gather | bytes 10240 | tf_op jit(solution)/shard_map/all_gather | solution.py:17
  110.2 1.7 pad.129
  111.9 0.7 add_bitcast_fusion.1
  112.6 7.2 %all-gather.2 = f32[4,1,512]{2,1,0:T(1,128)S(1)} all-gather(f32[1,1,512]{2,1,0:T(1,128)S(1)} %add_bitcast_fusion.1), channel_id=1, replica_groups=mesh['tp'=8,'seq'=4] {'seq'}, dimensions={0}, use_global_device_ids=true | all-gather | bytes 10240 | tf_op jit(solution)/shard_map/all_gather | solution.py:17
  120.0 8.6 %convolution_convert_fusion.1 = bf16[256,4096]{1,0:T(8,128)(2,1)} fusion(bf16[512,4096]{1,0:T(8,128)(2,1)} %param.29, bf16[4096,512]{1,0:T(8,128)(2,1)} %param.21, bf16[256,4096]{1,0:T(8,128)(2,1)} %param.18, f32[4096]{0:T(1024)S(1)} %copy-done.19, f32[256]{0:T(256)S(1)} %copy-done.17, f32[256,512]{1,0:T(8,128)} %pad.128, f32[256,512]{1,0:T(8,128)} %pad.129, ...), kind=kOutput, calls=%fused_computation.11 | convolution fusion | flops 2154561536 | bytes 14699520 | tf_op jit(solution)/shard_map/dot_general | solution.py:119
  128.9 151.3 %all-gather.7.cloned.1.call-done = bf16[2048,4096]{1,0:T(8,128)(2,1)} async-done(((bf16[256,4096]{1,0:T(8,128)(2,1)}), bf16[2048,4096]{1,0:T(8,128)(2,1)}) %all-gather.7.cloned.1.call-update) | async-done | bytes 16777232 | tf_op jit(solution)/shard_map/all_gather | solution.py:67
  280.2 10.5 %reduce_sum.43 = bf16[256,4096]{1,0:T(8,128)(2,1)} reduce(bf16[8,256,4096]{2,1,0:T(8,128)(2,1)} %bitcast.47, bf16[]{:T(256)} %constant.59.clone.1), dimensions={0}, to_apply=%region_3.4 | reduce | flops 7340032 | bytes 18874370 | tf_op jit(solution)/shard_map/reduce_sum | solution.py:67
  290.7 3.0 fusion.3
  294.2 0.8 copy-done.2
  295.0 2.0 fusion.6
  297.0 4.1 copy.44
  301.0 30.5 %all_to_all.19 = bf16[256,4,1024]{0,2,1:T(8,128)(2,1)} all-to-all(bf16[256,4,1024]{0,2,1:T(8,128)(2,1)} %bitcast.49), channel_id=1, replica_groups=mesh['tp'=8,'seq'=4] {'seq'}, dimensions={1} | all-to-all | bytes 4194304 | tf_op jit(solution)/shard_map/all_to_all | solution.py:123
  331.5 4.0 copy.45
  335.5 5.4 convolution_convert_fusion.2
  341.0 3.6 convolution_convert_fusion.3
  344.6 3.6 pad_maximum_fusion
  348.3 66.9 %reduce-scatter.2.cloned.1.call-done = bf16[256,3072]{1,0:T(8,128)(2,1)} async-done(((bf16[1024,3072]{1,0:T(8,128)(2,1)}), bf16[256,3072]{1,0:T(8,128)(2,1)}) %reduce-scatter.2.cloned.1.call-update) | async-done | bytes 1572880 | tf_op jit(solution)/shard_map/reduce_scatter | solution.py:35
  415.2 1.8 convert_element_type.70
  416.9 9.4 %convolution_convert_fusion = bf16[256,4096]{1,0:T(8,128)(2,1)} fusion(bf16[1536,4096]{1,0:T(8,128)(2,1)} %param.33, f32[256,3072]{1,0:T(8,128)S(1)} %convert_element_type.70), kind=kOutput, calls=%fused_computation.10 | convolution fusion | flops 3226206208 | bytes 17825792 | tf_op jit(solution)/shard_map/dot_general | solution.py:139
  426.4 151.2 %all-gather.9.cloned.1.call-done = bf16[2048,4096]{1,0:T(8,128)(2,1)} async-done(((bf16[256,4096]{1,0:T(8,128)(2,1)}), bf16[2048,4096]{1,0:T(8,128)(2,1)}) %all-gather.9.cloned.1.call-update) | async-done | bytes 16777232 | tf_op jit(solution)/shard_map/all_gather | solution.py:67
  577.6 10.6 %reduce_sum.45 = bf16[256,4096]{1,0:T(8,128)(2,1)} reduce(bf16[8,256,4096]{2,1,0:T(8,128)(2,1)} %bitcast.48, bf16[]{:T(256)} %constant.59.clone.1), dimensions={0}, to_apply=%region_6.7 | reduce | flops 7340032 | bytes 18874370 | tf_op jit(solution)/shard_map/reduce_sum | solution.py:67
  588.2 4.3 fusion.7
  (154 shorter events, 16.7 us)
Async XLA Ops:
  6.5 329.0 %copy-start = (bf16[1024,1536]{1,0:T(8,128)(2,1)S(1)}, bf16[1024,1536]{1,0:T(8,128)(2,1)}, u32[]{:S(2)}) copy-start(bf16[1024,1536]{1,0:T(8,128)(2,1)} %param.32) | copy-start | bytes 9437188
  6.5 273.6 %all-gather.7.cloned.1.call-start = ((), (), s32[]{:S(2)}) async-start(), calls=%async_computation.3 | async-start | bytes 18874368 | tf_op jit(solution)/shard_map/all_gather | solution.py:67
  8.8 4.2 copy-start.16
  8.8 9.1 %copy-start.14 = (f32[512]{0:T(512)S(1)}, f32[512]{0:T(512)}, u32[]{:S(2)}) copy-start(f32[512]{0:T(512)} %param.28) | copy-start | bytes 6148
  8.8 9.1 %copy-start.11 = (f32[4,512]{1,0:T(4,128)S(1)}, f32[4,512]{1,0:T(4,128)}, u32[]{:S(2)}) copy-start(f32[4,512]{1,0:T(4,128)} %param.22) | copy-start | bytes 24580
  8.8 10.5 %copy-start.15 = (f32[512]{0:T(512)S(1)}, f32[512]{0:T(512)}, u32[]{:S(2)}) copy-start(f32[512]{0:T(512)} %param.23) | copy-start | bytes 6148
  13.0 6.2 %collective-permute-start = (bf16[3,512]{1,0:T(4,128)(2,1)S(1)}, bf16[3,512]{1,0:T(4,128)(2,1)S(1)}, u32[]{:S(2)}, u32[]{:S(2)}) collective-permute-start(bf16[3,512]{1,0:T(4,128)(2,1)S(1)} %slice.356), channel_id=1, source_target_pairs={{0,1},{1,2},{2,3},{4,5},{5,6},{6,7},{8,9},{9,10},{10,11},{12,13},{... | collective-permute-start | bytes 9224 | tf_op jit(solution)/shard_map/ppermute | solution.py:12
  18.0 1.6 copy-start.7
  19.3 7.5 %copy-start.12 = (f32[512]{0:T(512)S(1)}, f32[512]{0:T(512)}, u32[]{:S(2)}) copy-start(f32[512]{0:T(512)} %param.25) | copy-start | bytes 6148
  19.3 7.5 %copy-start.13 = (f32[512]{0:T(512)S(1)}, f32[512]{0:T(512)}, u32[]{:S(2)}) copy-start(f32[512]{0:T(512)} %param.27) | copy-start | bytes 6148
  29.4 0.8 copy-start.3
  47.2 0.7 copy-start.5
  58.5 8.3 %copy-start.8 = (f32[31,512]{1,0:T(8,128)S(1)}, f32[31,512]{1,0:T(8,128)}, u32[]{:S(2)}) copy-start(f32[31,512]{1,0:T(8,128)} %slice.332) | copy-start | bytes 190468
  58.5 8.2 %copy-start.9 = (f32[31,512]{1,0:T(8,128)S(1)}, f32[31,512]{1,0:T(8,128)}, u32[]{:S(2)}) copy-start(f32[31,512]{1,0:T(8,128)} %slice.291) | copy-start | bytes 190468
  87.3 32.7 %copy-start.17 = (f32[256]{0:T(256)S(1)}, f32[256]{0:T(256)}, u32[]{:S(2)}) copy-start(f32[256]{0:T(256)} %copy-done.16) | copy-start | bytes 3076
  87.3 32.7 %copy-start.19 = (f32[4096]{0:T(1024)S(1)}, f32[4096]{0:T(1024)}, u32[]{:S(2)}) copy-start(f32[4096]{0:T(1024)} %param.19) | copy-start | bytes 49156
  89.4 20.8 %copy-start.6 = (f32[128,512]{1,0:T(8,128)S(1)}, f32[128,512]{1,0:T(8,128)}, u32[]{:S(2)}) copy-start(f32[128,512]{1,0:T(8,128)} %add.313) | copy-start | bytes 786436
  128.7 286.5 %reduce-scatter.2.cloned.1.call-start = ((), (), s32[]{:S(2)}) async-start(), calls=%async_computation.2 | async-start | bytes 7864320 | tf_op jit(solution)/shard_map/reduce_scatter | solution.py:35
  290.7 4.3 copy-start.10
  293.7 1.3 copy-start.2
  335.5 5.4 copy-start.4
  335.5 5.4 copy-start.18
  348.2 229.3 %all-gather.9.cloned.1.call-start = ((), (), s32[]{:S(2)}) async-start(), calls=%async_computation.4 | async-start | bytes 18874368 | tf_op jit(solution)/shard_map/all_gather | solution.py:67
  577.6 15.0 %copy-start.1 = (bf16[1024,1536]{1,0:T(8,128)(2,1)S(1)}, bf16[1024,1536]{1,0:T(8,128)(2,1)}, u32[]{:S(2)}) copy-start(bf16[1024,1536]{1,0:T(8,128)(2,1)} %param.32) | copy-start | bytes 9437188
Sparse Core Ops, SparseCore 0:
  128.8 151.3 all-gather.6
  348.4 66.7 reduce-scatter.1
  426.5 151.0 all-gather.8
